TPU v7x, 32 devices: a whole 2x2x4 slice. The times are simulated.
32 devices in a mesh: band: 16 (over z, x, core), ga: 2 (over y).
Axes of the slice: x: 2, y: 2, z: 4, core: 2. Of those that a mesh axis runs over, the one named last changes fastest.
Arguments:
- psi: float32 [2, 4096, 65536], P(None, 'band', 'ga'), may hold values from -0.0234375 to 0.0234375
- hx: float32 [2, 256, 65536], P(None, 'band', 'ga'), may hold values from -6 to 6
Outputs:
- h_sub: float32 [2, 4096, 256], P(None, ('band', 'ga'))
All inputs are finite; a program needn't handle non-finite values.
Results may differ from a plain program's by a relative error of at most 0.00007.
Values sent between devices are 32-bit elements; how exact they have to be, the bound alone decides.
A program may use at most 192 MiB of HBM per device.

v0:
```python
import jax
import jax.numpy as jnp
from jax import lax
from jax.sharding import PartitionSpec as P

SHARES = (22, 10)


def contract(left, right):
    return lax.dot_general(
        left,
        right,
        (((1,), (1,)), ((), ())),
        precision=lax.Precision.HIGH,
        preferred_element_type=jnp.float32,
    )


def per_device(psi, hx):
    parts, rows, depth = psi.shape
    unit = depth // sum(SHARES)
    bands = psi.reshape(parts * rows, depth)
    total = None
    first = 0
    pieces = []
    for share in SHARES:
        last = first + share * unit
        piece = lax.all_gather(hx[:, :, first:last], "band", axis=1, tiled=True)
        pieces.append((first, last, piece))
        first = last
    for first, last, piece in pieces:
        product = contract(bands[:, first:last], piece.reshape(-1, last - first))
        total = product if total is None else total + product
    vectors = total.shape[1] // parts
    real_left, imag_left = (total[:rows], total[rows:])
    real_tile = real_left[:, :vectors] + imag_left[:, vectors:]
    imag_tile = real_left[:, vectors:] - imag_left[:, :vectors]
    partial_value = jnp.stack([real_tile, imag_tile], axis=0)
    n = lax.axis_size("ga")
    me = lax.axis_index("ga")
    height = rows // n

    def block(owner):
        return lax.dynamic_slice_in_dim(partial_value, owner * height, height, axis=1)

    result = block(me)
    for step in range(1, n):
        ring = [(i, (i + step) % n) for i in range(n)]
        result = result + lax.ppermute(block(lax.rem(me + step, n)), "ga", ring)
    return result


def solution(mesh):
    in_specs = (P(None, "band", "ga"), P(None, "band", "ga"))
    out_specs = P(None, ("band", "ga"), None)
    return jax.shard_map(
        per_device, mesh=mesh, in_specs=in_specs, out_specs=out_specs, check_vma=False
    )
```

profile of v0, /device:TPU:0, one launch (start us, length us, event | category | flops | bytes accessed | tf_op | source)
XLA Modules:
  0.0 389.9 jit_solution(5589482113664164910)
XLA Ops:
  6.5 0.0 all-gather.3.cloned.1.call-start
  6.5 3.6 slice.31
  10.1 0.0 all-gather.3.cloned.1.call-update
  10.2 0.0 all-gather.5.cloned.1.call-start
  10.2 2.5 slice.33
  12.7 0.0 all-gather.5.cloned.1.call-update
  12.7 227.6 %all-gather.3.cloned.1.call-done = f32[2,256,22528]{2,1,0:T(8,128)} async-done(((f32[2,16,22528]{2,1,0:T(8,128)}), f32[2,256,22528]{2,1,0:T(8,128)}) %all-gather.3.cloned.1.call-update) | async-done | bytes 46137360 | tf_op jit(solution)/shard_map/all_gather | solution.py:28
  240.3 43.3 %fusion = f32[512,512]{1,0:T(8,128)S(1)} fusion(f32[512,22528]{1,0:T(8,128)} %bitcast.9, f32[512,32768]{1,0:T(8,128)} %bitcast), kind=kOutput, calls=%fused_computation | convolution fusion | flops 35433480192 | bytes 93323264 | tf_op jit(solution)/shard_map/dot_general | solution.py:10
  283.6 67.1 %all-gather.5.cloned.1.call-done = f32[2,256,10240]{2,1,0:T(8,128)} async-done(((f32[2,16,10240]{2,1,0:T(8,128)}), f32[2,256,10240]{2,1,0:T(8,128)}) %all-gather.5.cloned.1.call-update) | async-done | bytes 20971536 | tf_op jit(solution)/shard_map/all_gather | solution.py:28
  350.7 22.9 %fusion.4 = f32[512,512]{1,0:T(8,128)S(1)} fusion(f32[512,512]{1,0:T(8,128)S(1)} %fusion, f32[512,10240]{1,0:T(8,128)} %bitcast.10, f32[512,32768]{1,0:T(8,128)} %bitcast), kind=kOutput, calls=%fused_computation.4 | convolution fusion | flops 16106389504 | bytes 44040192 | tf_op jit(solution)/shard_map/dot_general | solution.py:10
  373.6 0.1 fusion.10
  373.8 1.5 collective-permute-start
  375.3 7.0 %collective-permute-done = f32[2,128,256]{2,1,0:T(8,128)S(1)} collective-permute-done((f32[2,128,256]{2,1,0:T(8,128)S(1)}, f32[2,128,256]{2,1,0:T(8,128)S(1)}, u32[]{:S(2)}, u32[]{:S(2)}) %collective-permute-start) | collective-permute-done | bytes 262176 | tf_op jit(solution)/shard_map/ppermute | solution.py:49
  382.3 0.7 fusion.9
  (1 shorter events, 0.0 us)
Async XLA Ops:
  6.5 233.8 %all-gather.3.cloned.1.call-start = ((), (), s32[]{:S(2)}) async-start(), calls=%async_computation | async-start | bytes 49020928 | tf_op jit(solution)/shard_map/all_gather | solution.py:28
  10.2 340.5 %all-gather.5.cloned.1.call-start = ((), (), s32[]{:S(2)}) async-start(), calls=%async_computation.1 | async-start | bytes 22282240 | tf_op jit(solution)/shard_map/all_gather | solution.py:28
  373.8 8.5 %collective-permute-start = (f32[2,128,256]{2,1,0:T(8,128)S(1)}, f32[2,128,256]{2,1,0:T(8,128)S(1)}, u32[]{:S(2)}, u32[]{:S(2)}) collective-permute-start(f32[2,128,256]{2,1,0:T(8,128)S(1)} %fusion.7), channel_id=1, source_target_pairs={{0,1},{1,0},{2,3},{3,2},{4,5},{5,4},{6,7},{7,6},{8,9},{9,8},{10,11... | collective-permute-start | bytes 786440 | tf_op jit(solution)/shard_map/ppermute | solution.py:49
Sparse Core Ops, SparseCore 0:
  10.3 230.0 all-gather.2
  241.9 108.7 all-gather.4
where the time goes:
time: 390 us
  waiting for transfers between devices  302 us (77%)
  matrix products  66.2 us (17%)
  between operations  13.4 us (3%)
  local copies, waits for them, and re-layouts  6.08 us (2%)
    all_gather x2, waiting for transfers between devices, per_device(): piece = lax.all_gather(hx[:, :, first:last], 'band', axis=1, tiled=True)  295 us
    dot_general x2, matrix products, contract(): lax.dot_general(left, right, (((1,), (1,)), ((), ())), precision=lax.Prec...  66.2 us
  transfers between devices with their start and end apart: 3, of which 3 were waited for; matrix products, arithmetic and copies ran while one was open for 12% of the time, Pallas kernels for 0%

commit v1 on v0

--- a/solution.py
+++ b/solution.py
@@ -2,6 +2,7 @@
 import jax.numpy as jnp
 from jax import lax
 from jax.sharding import PartitionSpec as P
+from jax.lax import all_gather
 
 SHARES = (22, 10)
 
@@ -25,7 +26,7 @@
     pieces = []
     for share in SHARES:
         last = first + share * unit
-        piece = lax.all_gather(hx[:, :, first:last], "band", axis=1, tiled=True)
+        piece = jnp.concatenate(all_gather(hx[:, :, first:last], "band"), 1)
         pieces.append((first, last, piece))
         first = last
     for first, last, piece in pieces:

time: 390 us -> 466 us (1.19)
  local copies, waits for them, and re-layouts: 6.08 us -> 55.7 us
  waiting for transfers between devices: 302 us -> 327 us
    reshape x0 -> x2, local copies, waits for them, and re-layouts: none -> 49.6 us  [per_device(): piece = jnp.concatenate(all_gather(hx[:, :, first:last], 'band'), 1)]
    all_gather x2, waiting for transfers between devices: 295 us -> 320 us  [per_device(): piece = jnp.concatenate(all_gather(hx[:, :, first:last], 'band'), 1)]
  transfers between devices with their start and end apart: 3 -> 3, of which waited for: 3 -> 3; matrix products, arithmetic and copies ran while one was open for 12% -> 4% of each run, Pallas kernels for 0% -> 0%
where the time goes in v1:
time: 466 us
  waiting for transfers between devices  327 us (70%)
  matrix products  66.5 us (14%)
  local copies, waits for them, and re-layouts  55.7 us (12%)
  between operations  13.4 us (3%)
    all_gather x2, waiting for transfers between devices, per_device(): piece = jnp.concatenate(all_gather(hx[:, :, first:last], 'band'), 1)  320 us
    dot_general x2, matrix products, contract(): lax.dot_general(left, right, (((1,), (1,)), ((), ())), precision=lax.Prec...  66.5 us
    reshape x2, local copies, waits for them, and re-layouts, per_device(): piece = jnp.concatenate(all_gather(hx[:, :, first:last], 'band'), 1)  49.6 us
  transfers between devices with their start and end apart: 3, of which 3 were waited for; matrix products, arithmetic and copies ran while one was open for 4% of the time, Pallas kernels for 0%

profile of v1, /device:TPU:0, one launch (start us, length us, event | category | flops | bytes accessed | tf_op | source)
XLA Modules:
  0.0 465.5 jit_solution(13488049225596107915)
XLA Ops:
  6.5 0.0 all-gather.7.cloned.1.call-start
  6.5 2.5 slice.33
  9.0 0.0 all-gather.7.cloned.1.call-update
  9.0 0.0 all-gather.5.cloned.1.call-start
  9.1 3.6 slice.31
  12.7 0.0 all-gather.5.cloned.1.call-update
  12.7 108.0 %all-gather.7.cloned.1.call-done = f32[32,16,10240]{2,1,0:T(8,128)} async-done(((f32[2,16,10240]{2,1,0:T(8,128)}), f32[32,16,10240]{2,1,0:T(8,128)}) %all-gather.7.cloned.1.call-update) | async-done | bytes 20971536 | tf_op jit(solution)/shard_map/all_gather | solution.py:29
  120.7 16.4 %copy.6 = f32[2,16,16,10240]{3,2,1,0:T(8,128)} copy(f32[2,16,16,10240]{3,2,0,1:T(8,128)} %bitcast.18) | data formatting | bytes 41943040 | tf_op jit(solution)/shard_map/reshape | solution.py:29
  137.1 212.5 %all-gather.5.cloned.1.call-done = f32[32,16,22528]{2,1,0:T(8,128)} async-done(((f32[2,16,22528]{2,1,0:T(8,128)}), f32[32,16,22528]{2,1,0:T(8,128)}) %all-gather.5.cloned.1.call-update) | async-done | bytes 46137360 | tf_op jit(solution)/shard_map/all_gather | solution.py:29
  349.6 33.2 %copy.5 = f32[2,16,16,22528]{3,2,1,0:T(8,128)} copy(f32[2,16,16,22528]{3,2,0,1:T(8,128)} %bitcast.17) | data formatting | bytes 92274688 | tf_op jit(solution)/shard_map/reshape | solution.py:29
  382.8 43.3 %fusion = f32[512,512]{1,0:T(8,128)S(1)} fusion(f32[512,22528]{1,0:T(8,128)} %bitcast.15, f32[512,32768]{1,0:T(8,128)} %bitcast), kind=kOutput, calls=%fused_computation | convolution fusion | flops 35433480192 | bytes 93323264 | tf_op jit(solution)/shard_map/dot_general | solution.py:11
  426.2 23.1 %fusion.4 = f32[512,512]{1,0:T(8,128)S(1)} fusion(f32[512,512]{1,0:T(8,128)S(1)} %fusion, f32[512,10240]{1,0:T(8,128)} %bitcast.16, f32[512,32768]{1,0:T(8,128)} %bitcast), kind=kOutput, calls=%fused_computation.4 | convolution fusion | flops 16106389504 | bytes 44040192 | tf_op jit(solution)/shard_map/dot_general | solution.py:11
  449.3 0.1 fusion.10
  449.4 1.5 collective-permute-start
  451.0 7.0 %collective-permute-done = f32[2,128,256]{2,1,0:T(8,128)S(1)} collective-permute-done((f32[2,128,256]{2,1,0:T(8,128)S(1)}, f32[2,128,256]{2,1,0:T(8,128)S(1)}, u32[]{:S(2)}, u32[]{:S(2)}) %collective-permute-start) | collective-permute-done | bytes 262176 | tf_op jit(solution)/shard_map/ppermute | solution.py:50
  458.0 0.7 fusion.9
  (1 shorter events, 0.0 us)
Async XLA Ops:
  6.5 114.2 %all-gather.7.cloned.1.call-start = ((), (), s32[]{:S(2)}) async-start(), calls=%async_computation.1 | async-start | bytes 22282240 | tf_op jit(solution)/shard_map/all_gather | solution.py:29
  9.0 340.6 %all-gather.5.cloned.1.call-start = ((), (), s32[]{:S(2)}) async-start(), calls=%async_computation | async-start | bytes 49020928 | tf_op jit(solution)/shard_map/all_gather | solution.py:29
  449.4 8.5 %collective-permute-start = (f32[2,128,256]{2,1,0:T(8,128)S(1)}, f32[2,128,256]{2,1,0:T(8,128)S(1)}, u32[]{:S(2)}, u32[]{:S(2)}) collective-permute-start(f32[2,128,256]{2,1,0:T(8,128)S(1)} %fusion.7), channel_id=1, source_target_pairs={{0,1},{1,0},{2,3},{3,2},{4,5},{5,4},{6,7},{7,6},{8,9},{9,8},{10,11... | collective-permute-start | bytes 786440 | tf_op jit(solution)/shard_map/ppermute | solution.py:50
Sparse Core Ops, SparseCore 0:
  9.2 111.4 all-gather.6
  122.3 227.2 all-gather.4
